TPU v7x, 32 devices: a whole 2x2x4 slice. The times are simulated.
32 devices in a mesh: grp: 4 (over y, x), blk: 8 (over z, core).
Axes of the slice: x: 2, y: 2, z: 4, core: 2. Of those that a mesh axis runs over, the one named last changes fastest.
Arguments:
- data: bfloat16 [256, 65536], P('blk'), may hold values from -8 to 8
- labels: int32 [256], P('blk'), may hold values from -1 to 1, as said below
- order: int32 [8, 4], P('blk'), may hold values from 0 to 3, each once within a row
- reg_index: int32 [4], P('grp'), parts along dimension 0, may hold values from 0 to 5
Outputs:
- dual: float32 [1024], P(('grp', 'blk')), parts along dimension 0
- margins: float32 [1024], P(('grp', 'blk')), parts along dimension 0
- gap: float32 [4], P('grp'), parts along dimension 0
There are 4 independent parts, one for each index of `grp`. A program takes and returns all parts, laid end to end along the dimension named above; an argument that names none is the same for every part. Nothing has to cross between parts.
Inputs may be any that keep to these rules, and one draw needn't show every extreme that they name: `labels`: each entry is -1 or 1.
All inputs are finite; a program needn't handle non-finite values.
Results may differ from a plain program's by a relative error of at most 0.00055.
Values sent between devices are 32-bit elements; how exact they have to be, the bound alone decides.
No kernel may reach another device: no remote copies, remote signals or barrier semaphores. Data moves between devices by JAX's collectives and lax.ppermute only.
A program may use at most 64 MiB of HBM per device.

v0:
```python
import math
import jax
import jax.numpy as jnp
from jax import lax
from jax.sharding import PartitionSpec as P

NBLOCKS = 4
ROUNDS = 2


def local_round(shard_data, signs, dual, order_row, weights, reg_total, sigma_prime, squared):
    block_rows = shard_data.shape[0] // NBLOCKS
    feature_scale = 1.0 / math.sqrt(shard_data.shape[1])
    local_weights = weights
    dual_change = jnp.zeros_like(dual)
    for position in range(NBLOCKS):
        offset = order_row[position] * block_rows
        block_data = lax.dynamic_slice_in_dim(shard_data, offset, block_rows, 0)
        block_signs = lax.dynamic_slice_in_dim(signs, offset, block_rows, 0)
        block_dual = lax.dynamic_slice_in_dim(dual, offset, block_rows, 0)
        block_change = lax.dynamic_slice_in_dim(dual_change, offset, block_rows, 0)
        block_norms = lax.dynamic_slice_in_dim(squared, offset, block_rows, 0)
        rounded = local_weights.astype(jnp.bfloat16)
        score = feature_scale * jnp.dot(block_data, rounded, preferred_element_type=jnp.float32)
        current = block_dual + block_change
        updated = jnp.clip(
            current + reg_total * (1.0 - block_signs * score) / (sigma_prime * block_norms),
            0.0,
            1.0,
        )
        change = updated - current
        dual_change = lax.dynamic_update_slice_in_dim(dual_change, block_change + change, offset, 0)
        coefficient = (block_signs * change).astype(jnp.bfloat16)
        local_weights = local_weights + sigma_prime * feature_scale / reg_total * jnp.dot(
            coefficient, block_data, preferred_element_type=jnp.float32
        )
    return dual_change


def shards(data, labels, order, reg_index):
    group_size = lax.axis_size("blk")
    row_count = data.shape[0]
    feature_count = data.shape[1]
    samples_all = row_count * group_size
    feature_scale = 1.0 / math.sqrt(feature_count)
    reg_strength = 0.04 * jnp.exp(0.5 * math.log(2.0) * reg_index[0].astype(jnp.float32))
    reg_total = reg_strength * samples_all
    sigma_prime = jnp.float32(group_size)
    signs = labels.astype(jnp.float32)
    squared = (
        jnp.einsum("rf,rf->r", data, data, preferred_element_type=jnp.float32) / feature_count
        + 1e-06
    )
    weights = jnp.zeros((feature_count,), jnp.float32)
    dual = jnp.zeros((row_count,), jnp.float32)
    for round_index in range(ROUNDS):
        dual_change = local_round(
            data, signs, dual, order[0], weights, reg_total, sigma_prime, squared
        )
        coefficient = (signs * dual_change).astype(jnp.bfloat16)
        delta = (
            feature_scale
            / reg_total
            * jnp.dot(coefficient, data, preferred_element_type=jnp.float32)
        )
        weights = weights + lax.psum(delta, "blk")
        dual = dual + dual_change
    margins = feature_scale * jnp.dot(
        data, weights.astype(jnp.bfloat16), preferred_element_type=jnp.float32
    )
    hinge = jnp.maximum(0.0, 1.0 - signs * margins)
    hinge_total, dual_total = lax.psum((jnp.sum(hinge), jnp.sum(dual)), "blk")
    gap = reg_strength * jnp.sum(weights * weights) + (hinge_total - dual_total) / samples_all
    return (dual, margins, gap.reshape(1))


def solution(mesh):
    placed = (P("blk", None), P("blk"), P("blk", None), P("grp"))
    return jax.shard_map(
        shards,
        mesh=mesh,
        in_specs=placed,
        out_specs=(P(("grp", "blk")), P(("grp", "blk")), P("grp")),
        check_vma=False,
    )
```

profile of v0, /device:TPU:0, one launch (start us, length us, event | category | flops | bytes accessed | tf_op | source)
XLA Modules:
  0.0 192.1 jit_solution(11065774794570149796)
XLA Ops:
  7.2 0.0 all-reduce.4.cloned.1.call-start
  7.2 1.4 fusion.134
  11.8 0.7 convert_element_type.59
  12.5 3.1 %fusion = f32[32]{0:T(128)S(1)} fusion(bf16[32,65536]{1,0:T(8,128)(2,1)} %param.4), kind=kLoop, calls=%fused_computation.1 | loop fusion | flops 6291424 | bytes 4194432 | tf_op jit(solution)/shard_map/rf,rf->r/dot_general | solution.py:51
  15.7 0.1 fusion.135
  15.7 2.1 %fusion.6 = f32[8]{0:T(128)S(1)} fusion(f32[8]{0:T(128)S(1)} %get-tuple-element.15, bf16[32,65536]{1,0:T(8,128)(2,1)} %param.4, s32[]{:T(128)S(6)} %select_n.8, f32[32]{0:T(128)S(1)} %multiply_add_fusion.3, f32[]{:T(128)} %bitcast), kind=kOutput, calls=%fused_computation.15 | convolution fusion | flops 1048632 | bytes 1050208 | tf_op jit(solution)/shard_map/dot_general | solution.py:24
  17.8 1.7 fusion.83
  19.5 0.2 dynamic_update_slice.24
  19.7 0.0 copy-start
  19.7 0.1 reshape.40
  19.9 2.2 %fusion.14 = f32[8]{0:T(128)S(1)} fusion(f32[8]{0:T(128)S(1)} %get-tuple-element.14, bf16[65536,1]{0,1:T(2,128)(2,1)S(1)} %reshape.40, bf16[32,65536]{1,0:T(8,128)(2,1)} %param.4, s32[]{:T(128)S(6)} %select_n.9, f32[32]{0:T(128)S(1)} %multiply_add_fusion.3, f32[]{:T(128)} %bitcast, f32[32]{0:T(128)S(1)} %dynamic_update_slice.24), kind=kOutput, calls=%fused_computation.23 | convolution fusion | flops 1048648 | bytes 1181312 | tf_op jit(solution)/shard_map/dot_general | solution.py:24
  22.1 0.0 copy-start.3
  22.1 0.2 add_dynamic-update-slice_fusion.3
  22.3 1.6 fusion.77
  24.0 0.1 reshape.44
  24.1 0.0 copy-done
  24.1 0.9 fusion.22
  25.0 0.2 add_dynamic-update-slice_fusion.2
  25.1 0.4 fusion.71
  25.6 0.1 add_convert_fusion.1
  25.7 0.1 reshape.48
  25.8 2.1 %fusion.31 = f32[8]{0:T(128)S(1)} fusion(bf16[65536,1]{0,1:T(2,128)(2,1)S(1)} %reshape.48, bf16[32,65536]{1,0:T(8,128)(2,1)} %param.4, s32[]{:T(128)S(6)} %select_n.11, f32[32]{0:T(128)S(1)} %add_dynamic-update-slice_fusion.2, f32[32]{0:T(128)S(1)} %multiply_add_fusion.3, f32[]{:T(128)} %bitcast, f32[32]{0:T(128)S(1)} %convert_element_type.59), kind=kOutput, calls=%fused_computation.40 | convolution fusion | flops 1048656 | bytes 1181312 | tf_op jit(solution)/shard_map/dot_general | solution.py:24
  27.9 0.2 dynamic_update_slice.27
  28.1 0.0 copy-done.3
  28.1 2.8 %fusion.108 = f32[1,65536]{1,0:T(1,128)S(1)} fusion(bf16[32,65536]{1,0:T(8,128)(2,1)} %param.4, f32[32]{0:T(128)S(1)} %dynamic_update_slice.27, s32[32]{0:T(128)S(1)} %copy-done.3), kind=kOutput, calls=%fused_computation.128 | convolution fusion | flops 4194400 | bytes 4456704 | tf_op jit(solution)/shard_map/dot_general | solution.py:64
  31.0 0.7 broadcast_multiply_fusion.1
  31.7 0.0 all-reduce.4.cloned.1.call-update
  31.7 0.0 all-reduce.6.cloned.1.call-start
  31.8 58.2 %all-reduce.4.cloned.1.call-done = f32[65536]{0:T(1024)} async-done(((f32[65536]{0:T(1024)}), f32[65536]{0:T(1024)}) %all-reduce.4.cloned.1.call-update) | async-done | bytes 262160 | tf_op jit(solution)/shard_map/psum | solution.py:66
  90.0 0.0 copy-start.2
  90.0 1.0 convert_element_type.68
  91.1 0.1 reshape.52
  91.2 2.1 %fusion.39 = f32[8]{0:T(128)S(1)} fusion(f32[8]{0:T(128)S(1)} %get-tuple-element.15, bf16[65536,1]{0,1:T(2,128)(2,1)S(1)} %reshape.52, bf16[32,65536]{1,0:T(8,128)(2,1)} %param.4, s32[]{:T(128)S(6)} %select_n.8, f32[32]{0:T(128)S(1)} %dynamic_update_slice.27, f32[32]{0:T(128)S(1)} %multiply_add_fusion.3, f32[]{:T(128)} %bitcast), kind=kOutput, calls=%fused_computation.48 | convolution fusion | flops 1048648 | bytes 1181312 | tf_op jit(solution)/shard_map/dot_general | solution.py:24
  93.3 1.7 fusion.80
  95.0 0.2 dynamic_update_slice.28
  95.2 0.0 copy-start.1
  95.2 1.1 fusion.87
  96.3 0.1 reshape.56
  96.5 2.1 %fusion.47 = f32[8]{0:T(128)S(1)} fusion(f32[8]{0:T(128)S(1)} %get-tuple-element.14, bf16[65536,1]{0,1:T(2,128)(2,1)S(1)} %reshape.56, bf16[32,65536]{1,0:T(8,128)(2,1)} %param.4, s32[]{:T(128)S(6)} %select_n.9, f32[32]{0:T(128)S(1)} %dynamic_update_slice.27, f32[32]{0:T(128)S(1)} %multiply_add_fusion.3, f32[]{:T(128)} %bitcast, f32[32]{0:T(128)S(1)} %dynamic_update_slice.28), kind=kOutput, calls=%fused_computation.56 | convolution fusion | flops 1048656 | bytes 1181344 | tf_op jit(solution)/shard_map/dot_general | solution.py:24
  98.6 0.2 add_dynamic-update-slice_fusion.1
  98.8 1.7 fusion.74
  100.4 0.0 copy-done.2
  100.5 0.1 reshape.60
  100.6 0.0 copy-done.1
  100.6 0.9 fusion.55
  101.5 0.2 add_dynamic-update-slice_fusion
  101.7 0.4 fusion.68
  102.1 0.1 add_convert_fusion
  102.2 0.1 reshape.64
  102.4 0.9 fusion.64
  103.2 0.2 dynamic_update_slice.31
  103.4 2.8 %fusion.103 = f32[1,65536]{1,0:T(1,128)S(1)} fusion(bf16[32,65536]{1,0:T(8,128)(2,1)} %param.4, f32[32]{0:T(128)S(1)} %dynamic_update_slice.31, s32[32]{0:T(128)S(1)} %copy-done.3), kind=kOutput, calls=%fused_computation.123 | convolution fusion | flops 4194400 | bytes 4456704 | tf_op jit(solution)/shard_map/dot_general | solution.py:64
  106.3 0.7 broadcast_multiply_fusion
  107.0 0.0 all-reduce.6.cloned.1.call-update
  107.0 1.1 fusion.133
  108.1 53.5 %all-reduce.6.cloned.1.call-done = f32[65536]{0:T(1024)} async-done(((f32[65536]{0:T(1024)}), f32[65536]{0:T(1024)}) %all-reduce.6.cloned.1.call-update) | async-done | bytes 262160 | tf_op jit(solution)/shard_map/psum | solution.py:66
  161.6 1.7 multiply_reduce_fusion
  163.3 0.1 reshape.68
  163.5 4.5 %maximum_reduce_fusion = (f32[]{:T(128)}, f32[32]{0:T(128)}) fusion(s32[32]{0:T(128)S(1)} %copy-done.3, bf16[65536,1]{0,1:T(2,128)(2,1)S(1)} %reshape.68, bf16[32,65536]{1,0:T(8,128)(2,1)} %param.4), kind=kOutput, calls=%fused_computation.133 | convolution fusion | flops 4194495 | bytes 4325636 | tf_op jit(solution)/shard_map/dot_general | solution.py:68
  168.0 14.3 %all-reduce = (f32[]{:T(128)}, f32[]{:T(128)}) all-reduce(f32[]{:T(128)} %get-tuple-element.16, f32[]{:T(128)} %get-tuple-element.5), channel_id=1, replica_groups=mesh['grp'=4,'blk'=8] {'blk'}, use_global_device_ids=true, to_apply=%region_4.5 | all-reduce | flops 2 | bytes 16 | tf_op jit(solution)/shard_map/psum | solution.py:72
  (6 shorter events, 0.1 us)
Async XLA Ops:
  7.2 82.9 %all-reduce.4.cloned.1.call-start = ((), (), s32[]{:S(2)}) async-start(), calls=%async_computation | async-start | bytes 524288 | tf_op jit(solution)/shard_map/psum | solution.py:66
  19.7 4.4 %copy-start = (bf16[32,65536]{1,0:T(8,128)(2,1)S(1)}, bf16[32,65536]{1,0:T(8,128)(2,1)}, u32[]{:S(2)}) copy-start(bf16[32,65536]{1,0:T(8,128)(2,1)} %param.4) | copy-start | bytes 12582916
  22.1 6.0 %copy-start.3 = (s32[32]{0:T(128)S(1)}, s32[32]{0:T(128)}, u32[]{:S(2)}) copy-start(s32[32]{0:T(128)} %param.5) | copy-start | bytes 388
  31.7 129.9 %all-reduce.6.cloned.1.call-start = ((), (), s32[]{:S(2)}) async-start(), calls=%async_computation.1 | async-start | bytes 524288 | tf_op jit(solution)/shard_map/psum | solution.py:66
  90.0 10.4 %copy-start.2 = (f32[65536]{0:T(1024)S(1)}, f32[65536]{0:T(1024)}, u32[]{:S(2)}) copy-start(f32[65536]{0:T(1024)} %all-reduce.4.cloned.1.call-done) | copy-start | bytes 786436
  95.2 5.4 %copy-start.1 = (bf16[32,65536]{1,0:T(8,128)(2,1)S(1)}, bf16[32,65536]{1,0:T(8,128)(2,1)}, u32[]{:S(2)}) copy-start(bf16[32,65536]{1,0:T(8,128)(2,1)} %param.4) | copy-start | bytes 12582916
Sparse Core Ops, SparseCore 0:
  31.8 58.1 all-reduce.3
  107.1 54.4 all-reduce.5
where the time goes:
time: 193 us; the launch traced here: 192 us
  waiting for transfers between devices  112 us (58%)
  matrix products  30.8 us (16%)
  between operations  20.5 us (11%)
  blocking collectives  14.3 us (7%)
  other arithmetic  11.1 us (6%)
  local copies, waits for them, and re-layouts  3.5 us (2%)
    psum x2, waiting for transfers between devices, shards(): weights = weights + lax.psum(delta, 'blk')  112 us
    psum x1, blocking collectives, shards(): hinge_total, dual_total = lax.psum((jnp.sum(hinge), jnp.sum(dual)), 'blk')  14.3 us
    dot_general x8, matrix products, local_round(): jnp.dot(block_data, rounded, preferred_element_type=jnp.float32)  13.1 us
    dot_general x6, matrix products, local_round(): jnp.dot(coefficient, block_data, preferred_element_type=jnp.float32)  7.46 us
    dot_general x2, matrix products, shards(): jnp.dot(coefficient, data, preferred_element_type=jnp.float32)  5.69 us
    dot_general x1, matrix products, shards(): jnp.dot(data, weights.astype(jnp.bfloat16), preferred_element_type=jnp.fl...  4.52 us
  transfers between devices with their start and end apart: 2, of which 2 were waited for; matrix products, arithmetic and copies ran while one was open for 1% of the time, Pallas kernels for 0%

commit v1 on v0

--- a/solution.py
+++ b/solution.py
@@ -63,7 +63,7 @@
             / reg_total
             * jnp.dot(coefficient, data, preferred_element_type=jnp.float32)
         )
-        weights = weights + lax.psum(delta, "blk")
+        weights = weights + jnp.sum(lax.all_gather(delta, "blk"), axis=0)
         dual = dual + dual_change
     margins = feature_scale * jnp.dot(
         data, weights.astype(jnp.bfloat16), preferred_element_type=jnp.float32

time: 193 us -> 148 us (0.77)
  waiting for transfers between devices: 112 us -> 59.6 us
  local copies, waits for them, and re-layouts: 3.5 us -> 7.5 us
  matrix products: 30.8 us -> 34.4 us
  other arithmetic: 11.1 us -> 9.1 us
    psum x2 -> x0, waiting for transfers between devices: 112 us -> none  [shards(): weights = weights + lax.psum(delta, 'blk')]
    all_gather x0 -> x2, waiting for transfers between devices: none -> 59.6 us  [shards(): weights = weights + jnp.sum(lax.all_gather(delta, 'blk'), axis=0)]
    all_gather x0 -> x2, local copies, waits for them, and re-layouts: none -> 3.93 us  [shards(): weights = weights + jnp.sum(lax.all_gather(delta, 'blk'), axis=0)]
    dot_general x8, matrix products: 13.1 us -> 15.5 us  [local_round(): jnp.dot(block_data, rounded, preferred_element_type=jnp.float32)]
    convert_element_type x7, other arithmetic: 2.38 us -> 0.25 us  [local_round(): rounded = local_weights.astype(jnp.bfloat16)]
where the time goes in v1:
time: 148 us; the launch traced here: 147 us
  waiting for transfers between devices  59.6 us (40%)
  matrix products  34.4 us (23%)
  between operations  20.8 us (14%)
  blocking collectives  15.9 us (11%)
  other arithmetic  9.1 us (6%)
  local copies, waits for them, and re-layouts  7.5 us (5%)
    all_gather x2, waiting for transfers between devices, shards(): weights = weights + jnp.sum(lax.all_gather(delta, 'blk'), axis=0)  59.6 us
    psum x1, blocking collectives, shards(): hinge_total, dual_total = lax.psum((jnp.sum(hinge), jnp.sum(dual)), 'blk')  15.9 us
    dot_general x8, matrix products, local_round(): jnp.dot(block_data, rounded, preferred_element_type=jnp.float32)  15.5 us
    dot_general x6, matrix products, local_round(): jnp.dot(coefficient, block_data, preferred_element_type=jnp.float32)  8.71 us
    dot_general x2, matrix products, shards(): jnp.dot(coefficient, data, preferred_element_type=jnp.float32)  5.69 us
    dot_general x1, matrix products, shards(): jnp.dot(data, weights.astype(jnp.bfloat16), preferred_element_type=jnp.fl...  4.49 us
    all_gather x2, local copies, waits for them, and re-layouts, shards(): weights = weights + jnp.sum(lax.all_gather(delta, 'blk'), axis=0)  3.93 us
    dot_general x1, other arithmetic, shards(): jnp.einsum('rf,rf->r', data, data, preferred_element_type=jnp.float32)  3.1 us
  transfers between devices with their start and end apart: 2, of which 2 were waited for; matrix products, arithmetic and copies ran while one was open for 1% of the time, Pallas kernels for 0%

profile of v1, /device:TPU:0, one launch (start us, length us, event | category | flops | bytes accessed | tf_op | source)
XLA Modules:
  0.0 147.4 jit_solution(1704334198066819783)
XLA Ops:
  7.2 0.0 all-gather.5.cloned.1.call-start
  7.2 1.5 %fusion.134 = (s32[1,1]{1,0:T(1,128)}, s32[1,1]{1,0:T(1,128)}, s32[1,1]{1,0:T(1,128)}, s32[1,1]{1,0:T(1,128)}) fusion(s32[1,4]{1,0:T(1,128)} %param.6), kind=kLoop, calls=%fused_computation.164 | loop fusion | bytes 32 | tf_op jit(solution)/shard_map/slice | solution.py:17
  10.7 0.7 convert_element_type.59
  12.0 3.1 %fusion = f32[32]{0:T(128)S(1)} fusion(bf16[32,65536]{1,0:T(8,128)(2,1)} %param.4), kind=kLoop, calls=%fused_computation.1 | loop fusion | flops 6291424 | bytes 4194432 | tf_op jit(solution)/shard_map/rf,rf->r/dot_general | solution.py:51
  15.2 0.1 fusion.135
  15.3 2.1 %fusion.6 = f32[8]{0:T(128)S(1)} fusion(f32[8]{0:T(128)S(1)} %get-tuple-element.15, bf16[32,65536]{1,0:T(8,128)(2,1)} %param.4, s32[]{:T(128)S(6)} %select_n.8, f32[32]{0:T(128)S(1)} %multiply_add_fusion.3, f32[]{:T(128)} %bitcast), kind=kOutput, calls=%fused_computation.15 | convolution fusion | flops 1048632 | bytes 1050208 | tf_op jit(solution)/shard_map/dot_general | solution.py:24
  17.3 1.7 %fusion.83 = f32[1,65536]{1,0:T(1,128)S(1)} fusion(bf16[32,65536]{1,0:T(8,128)(2,1)} %param.4, s32[]{:T(128)S(6)} %select_n.8, f32[8]{0:T(128)S(1)} %get-tuple-element.15, f32[8]{0:T(128)S(1)} %fusion.6), kind=kOutput, calls=%fused_computation.93 | convolution fusion | flops 1048592 | bytes 1310788 | tf_op jit(solution)/shard_map/dot_general | solution.py:34
  19.0 0.1 reshape.42
  19.2 0.2 dynamic_update_slice.24
  19.4 2.1 %fusion.14 = f32[8]{0:T(128)S(1)} fusion(f32[8]{0:T(128)S(1)} %get-tuple-element.14, bf16[65536,1]{0,1:T(2,128)(2,1)S(1)} %reshape.42, bf16[32,65536]{1,0:T(8,128)(2,1)} %param.4, s32[]{:T(128)S(6)} %select_n.9, f32[32]{0:T(128)S(1)} %multiply_add_fusion.3, f32[]{:T(128)} %bitcast, f32[32]{0:T(128)S(1)} %dynamic_update_slice.24), kind=kOutput, calls=%fused_computation.23 | convolution fusion | flops 1048648 | bytes 1181312 | tf_op jit(solution)/shard_map/dot_general | solution.py:24
  21.5 0.0 copy-start.1
  21.5 1.7 %fusion.77 = f32[1,65536]{1,0:T(1,128)S(1)} fusion(bf16[32,65536]{1,0:T(8,128)(2,1)} %param.4, s32[]{:T(128)S(6)} %select_n.9, f32[8]{0:T(128)S(1)} %get-tuple-element.14, f32[8]{0:T(128)S(1)} %fusion.14), kind=kOutput, calls=%fused_computation.87 | convolution fusion | flops 1048592 | bytes 1310788 | tf_op jit(solution)/shard_map/dot_general | solution.py:34
  23.2 0.2 add_dynamic-update-slice_fusion.3
  23.4 0.1 reshape.46
  23.5 2.1 %fusion.22 = f32[8]{0:T(128)S(1)} fusion(f32[8]{0:T(128)S(1)} %get-tuple-element.13, bf16[65536,1]{0,1:T(2,128)(2,1)S(1)} %reshape.46, bf16[32,65536]{1,0:T(8,128)(2,1)} %param.4, s32[]{:T(128)S(6)} %select_n.10, f32[32]{0:T(128)S(1)} %multiply_add_fusion.3, f32[]{:T(128)} %bitcast, f32[32]{0:T(128)S(1)} %add_dynamic-update-slice_fusion.3), kind=kOutput, calls=%fused_computation.31 | convolution fusion | flops 1048648 | bytes 1181312 | tf_op jit(solution)/shard_map/dot_general | solution.py:24
  25.6 1.7 %fusion.71 = f32[1,65536]{1,0:T(1,128)S(1)} fusion(bf16[32,65536]{1,0:T(8,128)(2,1)} %param.4, s32[]{:T(128)S(6)} %select_n.10, f32[8]{0:T(128)S(1)} %get-tuple-element.13, f32[8]{0:T(128)S(1)} %fusion.22), kind=kOutput, calls=%fused_computation.81 | convolution fusion | flops 1048592 | bytes 1310788 | tf_op jit(solution)/shard_map/dot_general | solution.py:34
  27.3 0.2 add_dynamic-update-slice_fusion.2
  28.1 0.1 add_convert_fusion.1
  28.2 0.1 reshape.50
  28.3 2.1 %fusion.31 = f32[8]{0:T(128)S(1)} fusion(bf16[65536,1]{0,1:T(2,128)(2,1)S(1)} %reshape.50, bf16[32,65536]{1,0:T(8,128)(2,1)} %param.4, s32[]{:T(128)S(6)} %select_n.11, f32[32]{0:T(128)S(1)} %add_dynamic-update-slice_fusion.2, f32[32]{0:T(128)S(1)} %multiply_add_fusion.3, f32[]{:T(128)} %bitcast, f32[32]{0:T(128)S(1)} %convert_element_type.59), kind=kOutput, calls=%fused_computation.40 | convolution fusion | flops 1048656 | bytes 1181312 | tf_op jit(solution)/shard_map/dot_general | solution.py:24
  30.4 0.2 dynamic_update_slice.27
  30.6 0.0 copy-done.1
  30.6 2.8 %fusion.108 = f32[1,65536]{1,0:T(1,128)S(1)} fusion(bf16[32,65536]{1,0:T(8,128)(2,1)} %param.4, f32[32]{0:T(128)S(1)} %dynamic_update_slice.27, s32[32]{0:T(128)S(1)} %copy-done.1), kind=kOutput, calls=%fused_computation.128 | convolution fusion | flops 4194400 | bytes 4456704 | tf_op jit(solution)/shard_map/dot_general | solution.py:64
  33.5 0.7 broadcast_multiply_fusion.1
  34.3 0.0 all-gather.5.cloned.1.call-update
  34.3 0.0 all-gather.7.cloned.1.call-start
  34.3 32.0 %all-gather.5.cloned.1.call-done = f32[524288]{0:T(1024)} async-done(((f32[65536]{0:T(1024)}), f32[524288]{0:T(1024)}) %all-gather.5.cloned.1.call-update) | async-done | bytes 2097168 | tf_op jit(solution)/shard_map/all_gather | solution.py:66
  66.3 2.0 %reshape.34 = f32[8,65536]{1,0:T(8,128)S(1)} reshape(f32[524288]{0:T(1024)} %all-gather.5.cloned.1.call-done) | data formatting | bytes 4194304 | tf_op jit(solution)/shard_map/all_gather | solution.py:66
  68.3 0.5 reduce_sum.45
  68.8 0.1 reshape.54
  68.9 2.1 %fusion.39 = f32[8]{0:T(128)S(1)} fusion(f32[8]{0:T(128)S(1)} %get-tuple-element.15, bf16[65536,1]{0,1:T(2,128)(2,1)S(1)} %reshape.54, bf16[32,65536]{1,0:T(8,128)(2,1)} %param.4, s32[]{:T(128)S(6)} %select_n.8, f32[32]{0:T(128)S(1)} %dynamic_update_slice.27, f32[32]{0:T(128)S(1)} %multiply_add_fusion.3, f32[]{:T(128)} %bitcast), kind=kOutput, calls=%fused_computation.48 | convolution fusion | flops 1048648 | bytes 1181312 | tf_op jit(solution)/shard_map/dot_general | solution.py:24
  71.0 1.7 %fusion.80 = f32[1,65536]{1,0:T(1,128)S(1)} fusion(bf16[32,65536]{1,0:T(8,128)(2,1)} %param.4, s32[]{:T(128)S(6)} %select_n.8, f32[8]{0:T(128)S(1)} %get-tuple-element.15, f32[8]{0:T(128)S(1)} %fusion.39), kind=kOutput, calls=%fused_computation.90 | convolution fusion | flops 1048592 | bytes 1310788 | tf_op jit(solution)/shard_map/dot_general | solution.py:34
  72.7 0.1 reshape.58
  72.9 0.2 dynamic_update_slice.28
  73.1 0.0 copy-start
  73.1 2.2 %fusion.47 = f32[8]{0:T(128)S(1)} fusion(f32[8]{0:T(128)S(1)} %get-tuple-element.14, bf16[65536,1]{0,1:T(2,128)(2,1)S(1)} %reshape.58, bf16[32,65536]{1,0:T(8,128)(2,1)} %param.4, s32[]{:T(128)S(6)} %select_n.9, f32[32]{0:T(128)S(1)} %dynamic_update_slice.27, f32[32]{0:T(128)S(1)} %multiply_add_fusion.3, f32[]{:T(128)} %bitcast, f32[32]{0:T(128)S(1)} %dynamic_update_slice.28), kind=kOutput, calls=%fused_computation.56 | convolution fusion | flops 1048656 | bytes 1181344 | tf_op jit(solution)/shard_map/dot_general | solution.py:24
  75.3 1.7 %fusion.74 = f32[1,65536]{1,0:T(1,128)S(1)} fusion(bf16[32,65536]{1,0:T(8,128)(2,1)} %param.4, s32[]{:T(128)S(6)} %select_n.9, f32[8]{0:T(128)S(1)} %get-tuple-element.14, f32[8]{0:T(128)S(1)} %fusion.47), kind=kOutput, calls=%fused_computation.84 | convolution fusion | flops 1048592 | bytes 1310788 | tf_op jit(solution)/shard_map/dot_general | solution.py:34
  77.0 0.2 add_dynamic-update-slice_fusion.1
  77.2 0.1 reshape.62
  77.4 2.1 %fusion.55 = f32[8]{0:T(128)S(1)} fusion(f32[8]{0:T(128)S(1)} %get-tuple-element.13, bf16[65536,1]{0,1:T(2,128)(2,1)S(1)} %reshape.62, bf16[32,65536]{1,0:T(8,128)(2,1)} %param.4, s32[]{:T(128)S(6)} %select_n.10, f32[32]{0:T(128)S(1)} %dynamic_update_slice.27, f32[32]{0:T(128)S(1)} %multiply_add_fusion.3, f32[]{:T(128)} %bitcast, ...), kind=kOutput, calls=%fused_computation.64 | convolution fusion | flops 1048656 | bytes 1181344 | tf_op jit(solution)/shard_map/dot_general | solution.py:24
  79.4 0.0 copy-done
  79.4 0.4 fusion.68
  79.9 0.2 add_dynamic-update-slice_fusion
  80.1 0.1 add_convert_fusion
  80.2 0.1 reshape.66
  80.3 0.9 fusion.64
  81.2 0.2 dynamic_update_slice.31
  81.4 2.8 %fusion.103 = f32[1,65536]{1,0:T(1,128)S(1)} fusion(bf16[32,65536]{1,0:T(8,128)(2,1)} %param.4, f32[32]{0:T(128)S(1)} %dynamic_update_slice.31, s32[32]{0:T(128)S(1)} %copy-done.1), kind=kOutput, calls=%fused_computation.123 | convolution fusion | flops 4194400 | bytes 4456704 | tf_op jit(solution)/shard_map/dot_general | solution.py:64
  84.2 0.7 broadcast_multiply_fusion
  85.0 0.0 all-gather.7.cloned.1.call-update
  85.0 1.1 fusion.133
  86.1 27.6 %all-gather.7.cloned.1.call-done = f32[524288]{0:T(1024)} async-done(((f32[65536]{0:T(1024)}), f32[524288]{0:T(1024)}) %all-gather.7.cloned.1.call-update) | async-done | bytes 2097168 | tf_op jit(solution)/shard_map/all_gather | solution.py:66
  113.7 2.0 %reshape.35 = f32[8,65536]{1,0:T(8,128)S(1)} reshape(f32[524288]{0:T(1024)} %all-gather.7.cloned.1.call-done) | data formatting | bytes 4194304 | tf_op jit(solution)/shard_map/all_gather | solution.py:66
  115.7 0.5 reduce_sum.46
  116.2 0.7 multiply_reduce_fusion
  116.9 0.1 reshape.70
  117.1 4.5 %maximum_reduce_fusion = (f32[]{:T(128)}, f32[32]{0:T(128)}) fusion(s32[32]{0:T(128)S(1)} %copy-done.1, bf16[65536,1]{0,1:T(2,128)(2,1)S(1)} %reshape.70, bf16[32,65536]{1,0:T(8,128)(2,1)} %param.4), kind=kOutput, calls=%fused_computation.133 | convolution fusion | flops 4194495 | bytes 4325636 | tf_op jit(solution)/shard_map/dot_general | solution.py:68
  121.5 15.9 %all-reduce = (f32[]{:T(128)}, f32[]{:T(128)}) all-reduce(f32[]{:T(128)} %get-tuple-element.16, f32[]{:T(128)} %get-tuple-element.5), channel_id=1, replica_groups=mesh['grp'=4,'blk'=8] {'blk'}, use_global_device_ids=true, to_apply=%region_4.5 | all-reduce | flops 2 | bytes 16 | tf_op jit(solution)/shard_map/psum | solution.py:72
  (8 shorter events, 0.2 us)
Async XLA Ops:
  7.2 59.1 %all-gather.5.cloned.1.call-start = ((), (), s32[]{:S(2)}) async-start(), calls=%async_computation | async-start | bytes 2359296 | tf_op jit(solution)/shard_map/all_gather | solution.py:66
  21.5 9.1 %copy-start.1 = (s32[32]{0:T(128)S(1)}, s32[32]{0:T(128)}, u32[]{:S(2)}) copy-start(s32[32]{0:T(128)} %param.5) | copy-start | bytes 388
  34.3 79.4 %all-gather.7.cloned.1.call-start = ((), (), s32[]{:S(2)}) async-start(), calls=%async_computation.1 | async-start | bytes 2359296 | tf_op jit(solution)/shard_map/all_gather | solution.py:66
  73.1 6.3 %copy-start = (bf16[32,65536]{1,0:T(8,128)(2,1)S(1)}, bf16[32,65536]{1,0:T(8,128)(2,1)}, u32[]{:S(2)}) copy-start(bf16[32,65536]{1,0:T(8,128)(2,1)} %param.4) | copy-start | bytes 12582916
Sparse Core Ops, SparseCore 0:
  34.4 31.8 all-gather.4
  85.1 28.5 all-gather.6
